TPU v7x, 32 devices: a whole 2x2x4 slice. The times are simulated.
32 devices in a mesh: groups: 1, ep: 8 (over z, y), tp: 2 (over x), sub: 2 (over core).
Axes of the slice: x: 2, y: 2, z: 4, core: 2. Of those that a mesh axis runs over, the one named last changes fastest.
Arguments:
- queries: bfloat16 [128, 64, 128], P(('groups', 'ep', 'sub'), 'tp'), may hold values from -80 to 80
- new_keys: bfloat16 [128, 4, 128], P(('groups', 'ep', 'sub'), 'tp'), may hold values from -4 to 4
- new_values: bfloat16 [128, 4, 128], P(('groups', 'ep', 'sub'), 'tp'), may hold values from -5 to 5
- key_codes: int32 [128, 4, 8, 128], P(('groups', 'ep', 'sub'), 'tp'), may hold values from -2147483648 to 2147483647, as said below
- key_scale: bfloat16 [128, 4, 4, 128], P(('groups', 'ep', 'sub'), 'tp'), may hold values from 0.19921875 to 1
- key_zero: bfloat16 [128, 4, 4, 128], P(('groups', 'ep', 'sub'), 'tp'), may hold values from -1.5 to 0.5
- value_codes: int32 [128, 4, 8, 128], P(('groups', 'ep', 'sub'), 'tp'), may hold values from -2147483648 to 2147483647, as said below
- value_scale: bfloat16 [128, 4, 128], P(('groups', 'ep', 'sub'), 'tp'), may hold values from 0.19921875 to 1
- value_zero: bfloat16 [128, 4, 128], P(('groups', 'ep', 'sub'), 'tp'), may hold values from -1.1953125 to 0.19921875
- lengths: int32 [128], P(('groups', 'ep', 'sub')), may hold values from 1 to 128, as said below
- out_weight: bfloat16 [8192, 2048], P('tp', ('ep', 'sub')), may hold values from -0.0625 to 0.0625
- residual: bfloat16 [128, 2048], P(('groups', 'ep', 'sub'), 'tp'), may hold values from -8 to 8
- norm_gain: bfloat16 [2048], P('tp'), may hold values from 0.099609375 to 1.8984375
- expert_ids: int32 [128, 8], P(('groups', 'ep', 'sub')), may hold values from 0 to 15, all different within a row; in each aligned block of 8 rows (0 to 7, 8 to 15, ...) at most 8 rows name the same one
- route_weights: int32 [128, 8], P(('groups', 'ep', 'sub')), may hold values from 1 to 65535
- capacity: int32 [16], P('groups'), may hold values from 16 to 32, as said below
- w_gate: bfloat16 [16, 2048, 768], P(('ep', 'sub'), 'tp'), may hold values from -0.125 to 0.125
- w_up: bfloat16 [16, 2048, 768], P(('ep', 'sub'), 'tp'), may hold values from -0.125 to 0.125
- w_down: bfloat16 [16, 768, 2048], P(('ep', 'sub'), None, 'tp'), may hold values from -0.21875 to 0.21875
Outputs:
- mixed: bfloat16 [128, 2048], P(('groups', 'ep', 'sub'), 'tp')
Inputs may be any that keep to these rules, and one draw needn't show every extreme that they name: `key_codes`: each word holds 16 two-bit codes: position 16 w + j in bits 2 j and 2 j + 1 of word w. `value_codes`: packed as key_codes. `lengths`: some request of the batch has exactly 128 cached positions. `expert_ids`: each row names 8 different experts; within the rows of one device (aligned blocks of 8 rows) no expert is named by more than 8 rows, and that bound is reached. Several experts have capacity 32.
All inputs are finite; a program needn't handle non-finite values.
Results may differ from a plain program's by a relative error of at most 0.014.
Values may be sent and summed in bfloat16 or wider, within the bound.
A program may use at most 64 MiB of HBM per device.

v0:
```python
import math

import jax
import jax.numpy as jnp
from jax import lax
from jax.sharding import PartitionSpec as P

EPS = 1e-06


def carried_in(value, axis, join, neutral):
    count, mine = (lax.axis_size(axis), lax.axis_index(axis))
    pieces = lax.all_gather(value, axis)
    total = jnp.full_like(value, 0) + jnp.asarray(neutral, value.dtype)

    def turn(position, total):
        longer = join(total, pieces[position])
        return jnp.where(position < mine, longer, total)

    return lax.fori_loop(0, count - 1, turn, total)


def unpack_codes(packed_words):
    shifts = 2 * jnp.arange(16)
    code_vals = jnp.bitwise_and(jnp.right_shift(packed_words[..., None, :], shifts[:, None]), 3)
    word_shape = packed_words.shape
    return code_vals.reshape(word_shape[:-2] + (word_shape[-2] * 16, word_shape[-1])).astype(
        jnp.float32
    )


def attend_one(request_data):
    (
        query_heads,
        key_new,
        value_new,
        key_words,
        key_step,
        key_offset,
        value_words,
        value_step,
        value_offset,
        seq_length,
    ) = request_data
    kv_heads, head_dim = key_new.shape
    token_group = key_words.shape[1] * 16 // key_step.shape[1]
    keys_deq = unpack_codes(key_words) * jnp.repeat(
        key_step.astype(jnp.float32), token_group, axis=1
    )
    keys_deq = (keys_deq + jnp.repeat(key_offset.astype(jnp.float32), token_group, axis=1)).astype(
        jnp.bfloat16
    )
    values_deq = (
        unpack_codes(value_words) * value_step.astype(jnp.float32)[:, :, None]
        + value_offset.astype(jnp.float32)[:, :, None]
    )
    values_deq = values_deq.astype(jnp.bfloat16)
    grouped = query_heads.reshape(kv_heads, -1, head_dim)
    inv_scale = 1.0 / math.sqrt(head_dim)
    scores = (
        jnp.einsum("kgd,kld->kgl", grouped, keys_deq, preferred_element_type=jnp.float32)
        * inv_scale
    )
    own_score = (
        jnp.einsum("kgd,kd->kg", grouped, key_new, preferred_element_type=jnp.float32) * inv_scale
    )
    usable = jnp.arange(keys_deq.shape[1]) < seq_length
    scores = jnp.where(usable, scores, -jnp.inf)
    highest = jnp.maximum(jnp.max(scores, axis=2), own_score)
    weights = jnp.exp(scores - highest[:, :, None])
    own_weight = jnp.exp(own_score - highest)
    totals = jnp.sum(weights, axis=2) + own_weight
    weights = (weights / totals[:, :, None]).astype(jnp.bfloat16)
    own_weight = (own_weight / totals).astype(jnp.bfloat16)
    result = jnp.einsum("kgl,kld->kgd", weights, values_deq, preferred_element_type=jnp.float32)
    result = (
        result
        + own_weight.astype(jnp.float32)[:, :, None] * value_new.astype(jnp.float32)[:, None, :]
    )
    return result.reshape(-1).astype(jnp.bfloat16)


def expert_ffn(packed_rows, w_gate, w_up, w_down, tensor_sum):
    gate_sum = jnp.dot(packed_rows, w_gate[0], preferred_element_type=jnp.float32)
    up_sum = jnp.dot(packed_rows, w_up[0], preferred_element_type=jnp.float32)
    gate_sum, up_sum = tensor_sum(gate_sum, up_sum)
    activated = (jax.nn.silu(gate_sum) * up_sum).astype(jnp.bfloat16)
    return jnp.dot(activated, w_down[0], preferred_element_type=jnp.float32).astype(jnp.bfloat16)


def add_counts(earlier, later):
    return earlier + later


def shards(
    queries,
    new_keys,
    new_values,
    key_codes,
    key_scale,
    key_zero,
    value_codes,
    value_scale,
    value_zero,
    lengths,
    out_weight,
    residual,
    norm_gain,
    expert_ids,
    route_weights,
    capacity,
    w_gate,
    w_up,
    w_down,
):
    attended = lax.map(
        attend_one,
        (
            queries,
            new_keys,
            new_values,
            key_codes,
            key_scale,
            key_zero,
            value_codes,
            value_scale,
            value_zero,
            lengths,
        ),
    )
    spread = jnp.dot(
        lax.all_gather(attended, ("ep", "sub"), axis=0, tiled=True),
        out_weight,
        preferred_element_type=jnp.float32,
    )
    partial_sum = lax.all_to_all(
        spread.astype(jnp.bfloat16), ("ep", "sub"), split_axis=0, concat_axis=1, tiled=True
    ).astype(spread.dtype)
    quarter = residual.shape[1]
    tp_index = lax.axis_index("tp")
    own_cols = lax.dynamic_slice_in_dim(
        partial_sum, tp_index * quarter, quarter, 1
    ) + residual.astype(jnp.float32)
    placed = lax.dynamic_update_slice_in_dim(partial_sum, own_cols, tp_index * quarter, 1)
    hidden_full = lax.psum(placed.astype(jnp.bfloat16), "tp").astype(jnp.float32)
    hidden_state = lax.dynamic_slice_in_dim(hidden_full, tp_index * quarter, quarter, 1)
    mean_square = jnp.mean(hidden_full * hidden_full, axis=1, keepdims=True)
    normed = (hidden_state * lax.rsqrt(mean_square + EPS) * norm_gain.astype(jnp.float32)).astype(
        jnp.bfloat16
    )
    requests, top_count = expert_ids.shape
    experts_all = capacity.shape[0]
    slot_rows = min(requests, max(2, 5 * requests * top_count // (2 * experts_all)))
    chosen = (expert_ids[:, :, None] == jnp.arange(experts_all, dtype=jnp.int32)).astype(jnp.int32)
    is_named = jnp.sum(chosen, axis=1)
    local_rank = jnp.cumsum(is_named, axis=0) - is_named
    counts = jnp.sum(is_named, axis=0)
    raw_weight = route_weights.astype(jnp.float32)
    shares = raw_weight / jnp.sum(raw_weight, axis=1, keepdims=True)
    weight_per = jnp.sum(chosen.astype(jnp.float32) * shares[:, :, None], axis=1)
    slot_ids = jnp.arange(slot_rows, dtype=jnp.int32)
    at_slot = (local_rank[:, :, None] == slot_ids) & (is_named[:, :, None] > 0)
    offsets = carried_in(counts, ("ep", "sub"), add_counts, jnp.zeros_like(counts))
    kept_rows = offsets[None, :] + local_rank < capacity[None, :]
    send_map = (at_slot & kept_rows[:, :, None]).astype(jnp.bfloat16).reshape(requests, -1)
    outgoing = jnp.dot(send_map.T, normed, preferred_element_type=jnp.float32).astype(jnp.bfloat16)
    outgoing = outgoing.reshape(experts_all, slot_rows, quarter)

    def slot_sums(gate_sum, up_sum):
        return (
            lax.psum(gate_sum.astype(jnp.bfloat16), "tp").astype(jnp.float32),
            lax.psum(up_sum.astype(jnp.bfloat16), "tp").astype(jnp.float32),
        )

    received = lax.all_to_all(outgoing, ("ep", "sub"), split_axis=0, concat_axis=0, tiled=True)
    source_count, item_count, width = received.shape
    expert_out = expert_ffn(received.reshape(-1, width), w_gate, w_up, w_down, slot_sums)
    returned = lax.all_to_all(
        expert_out.reshape(source_count, item_count, width),
        ("ep", "sub"),
        split_axis=0,
        concat_axis=0,
        tiled=True,
    )
    combine_map = (at_slot.astype(jnp.float32) * weight_per[:, :, None]).reshape(requests, -1)
    moe = jnp.dot(
        combine_map,
        returned.reshape(-1, quarter).astype(jnp.float32),
        precision=lax.Precision.HIGHEST,
    )
    return (hidden_state + moe).astype(jnp.bfloat16)


def solution(mesh):
    return jax.shard_map(
        shards,
        mesh=mesh,
        in_specs=(
            P(("groups", "ep", "sub"), "tp", None),
            P(("groups", "ep", "sub"), "tp", None),
            P(("groups", "ep", "sub"), "tp", None),
            P(("groups", "ep", "sub"), "tp", None, None),
            P(("groups", "ep", "sub"), "tp", None, None),
            P(("groups", "ep", "sub"), "tp", None, None),
            P(("groups", "ep", "sub"), "tp", None, None),
            P(("groups", "ep", "sub"), "tp", None),
            P(("groups", "ep", "sub"), "tp", None),
            P(("groups", "ep", "sub")),
            P("tp", ("ep", "sub")),
            P(("groups", "ep", "sub"), "tp"),
            P("tp"),
            P(("groups", "ep", "sub"), None),
            P(("groups", "ep", "sub"), None),
            P("groups"),
            P(("ep", "sub"), "tp", None),
            P(("ep", "sub"), "tp", None),
            P(("ep", "sub"), None, "tp"),
        ),
        out_specs=P(("groups", "ep", "sub"), "tp"),
        check_vma=False,
    )
```

profile of v0, /device:TPU:0, one launch (start us, length us, event | category | flops | bytes accessed | tf_op | source)
XLA Modules:
  0.0 192.8 jit_solution(8907037940047860331)
XLA Ops:
  6.6 59.3 %while.24 = (s32[]{:T(128)}, bf16[8,4096]{1,0:T(8,128)(2,1)S(1)}, s32[8]{0:T(128)}, bf16[8,32,128]{2,1,0:T(8,128)(2,1)}, s32[8,2,8,128]{3,2,1,0:T(8,128)}, /*ind...) while((s32[]{:T(128)}, bf16[8,4096]{1,0:T(8,128)(2,1)S(1)}, ...), condition=%wide.region_3.4_spmd, body=%wide.region_0.3_spmd.sunk | while | flops 2546802 | bytes 468409 | solution.py:116
  6.6 0.8 fusion.100
  7.5 0.7 dynamic-slice_bitcast_fusion.3
  9.7 1.3 dynamic_slice.101
  14.9 0.7 dynamic-slice_bitcast_fusion.3
  17.1 1.3 dynamic_slice.101
  22.3 0.7 dynamic-slice_bitcast_fusion.3
  24.5 1.3 dynamic_slice.101
  29.7 0.7 dynamic-slice_bitcast_fusion.3
  31.9 1.3 dynamic_slice.101
  37.1 0.7 dynamic-slice_bitcast_fusion.3
  39.3 1.3 dynamic_slice.101
  44.5 0.7 dynamic-slice_bitcast_fusion.3
  46.7 1.3 dynamic_slice.101
  51.9 0.7 dynamic-slice_bitcast_fusion.3
  54.1 1.3 dynamic_slice.101
  59.3 0.7 dynamic-slice_bitcast_fusion.3
  61.5 1.3 dynamic_slice.101
  68.0 13.8 %all-reduce = s32[256]{0:T(256)S(1)} all-reduce(s32[256]{0:T(256)S(1)} %dynamic-update-slice), channel_id=2, replica_groups=mesh['groups'=1,'ep'=8,'tp'=2,'sub'=2] {'ep','sub'}, use_global_device_ids=true, to_apply=%add | all-reduce | flops 256 | bytes 2048
  82.5 24.7 %all-gather.3.cloned.1.call-done = bf16[128,4096]{1,0:T(8,128)(2,1)} async-done(((bf16[8,4096]{1,0:T(8,128)(2,1)}), bf16[128,4096]{1,0:T(8,128)(2,1)}) %all-gather.3.cloned.1.call-update) | async-done | bytes 1048592 | tf_op jit(solution)/shard_map/all_gather | solution.py:132
  107.2 2.6 %fusion.47 = bf16[16,8,128]{2,1,0:T(8,128)(2,1)} fusion(bf16[128,4096]{1,0:T(8,128)(2,1)} %all-gather.3.cloned.1.call-done, bf16[4096,128]{1,0:T(8,128)(2,1)} %param.33), kind=kOutput, calls=%fused_computation.65 | convolution fusion | flops 134234112 | bytes 2129920 | tf_op jit(solution)/shard_map/dot_general | solution.py:131
  109.8 3.7 %all-to-all-start = ((bf16[16,8,128]{2,1,0:T(8,128)(2,1)}), bf16[16,8,128]{2,1,0:T(8,128)(2,1)S(1)}, u32[]{:S(2)}, u32[]{:S(2)}) async-start(bf16[16,8,128]{2,1,0:T(8,128)(2,1)} %fusion.47), calls=%async_computation | async-start | bytes 65536 | tf_op jit(solution)/shard_map/all_to_all | solution.py:136
  114.3 5.9 %all-to-all-done = bf16[16,8,128]{2,1,0:T(8,128)(2,1)S(1)} async-done(((bf16[16,8,128]{2,1,0:T(8,128)(2,1)}), bf16[16,8,128]{2,1,0:T(8,128)(2,1)S(1)}, u32[]{:S(2)}, u32[]{:S(2)}) %all-to-all-start) | async-done | bytes 32800 | tf_op jit(solution)/shard_map/all_to_all | solution.py:136
  120.2 8.4 %psum.21 = bf16[8,2048]{1,0:T(8,128)(2,1)S(1)} all-reduce(bf16[8,2048]{1,0:T(8,128)(2,1)S(1)} %convert_element_type.144), channel_id=1, replica_groups=mesh['groups'=1,'ep'=8,'tp'=2,'sub'=2] {'tp'}, use_global_device_ids=true, to_apply=%region_4.5 | all-reduce | flops 16384 | bytes 65536 | tf_op jit(solution)/shard_map/psum | solution.py:145
  129.0 12.6 %all_to_all.23 = bf16[16,8,1024]{2,1,0:T(8,128)(2,1)S(1)} all-to-all(bf16[16,8,1024]{2,1,0:T(8,128)(2,1)S(1)} %fusion.43), channel_id=1, replica_groups=mesh['groups'=1,'ep'=8,'tp'=2,'sub'=2] {'ep','sub'}, dimensions={0} | all-to-all | bytes 524288 | tf_op jit(solution)/shard_map/all_to_all | solution.py:175
  141.6 1.1 fusion.40
  142.7 1.0 fusion.37
  143.9 23.1 %all-reduce.4.cloned.1.call-done = (bf16[128,768]{1,0:T(8,128)(2,1)}, bf16[128,768]{1,0:T(8,128)(2,1)}) async-done(((bf16[128,768]{1,0:T(8,128)(2,1)}, bf16[128,768]{1,0:T(8,128)(2,1)}), (bf16[128,768]{1,0:T(8,128)(2,1)}, bf16[128,768]{1,0:T(8,128)(2,1)})) %all-reduce.4.cloned.1.call-update) | async-done | bytes 393232 | tf_op jit(solution)/shard_map/psum | solution.py:172
  167.0 2.1 %fusion.44 = bf16[16,8,1024]{2,1,0:T(8,128)(2,1)} fusion(bf16[1,768,1024]{2,1,0:T(8,128)(2,1)S(1)} %copy-done, bf16[128,768]{1,0:T(8,128)(2,1)} %get-tuple-element.197, bf16[128,768]{1,0:T(8,128)(2,1)} %get-tuple-element.198), kind=kOutput, calls=%fused_computation.63 | convolution fusion | flops 202244096 | bytes 2228224 | tf_op jit(solution)/shard_map/dot_general | solution.py:88
  169.1 5.6 %all-to-all-start.2 = ((bf16[16,8,1024]{2,1,0:T(8,128)(2,1)}), bf16[16,8,1024]{2,1,0:T(8,128)(2,1)S(1)}, u32[]{:S(2)}, u32[]{:S(2)}) async-start(bf16[16,8,1024]{2,1,0:T(8,128)(2,1)} %fusion.44), calls=%async_computation.2 | async-start | bytes 524288 | tf_op jit(solution)/shard_map/all_to_all | solution.py:178
  175.0 9.7 %all-to-all-done.2 = bf16[16,8,1024]{2,1,0:T(8,128)(2,1)S(1)} async-done(((bf16[16,8,1024]{2,1,0:T(8,128)(2,1)}), bf16[16,8,1024]{2,1,0:T(8,128)(2,1)S(1)}, u32[]{:S(2)}, u32[]{:S(2)}) %all-to-all-start.2) | async-done | bytes 262176 | tf_op jit(solution)/shard_map/all_to_all | solution.py:178
  184.7 1.2 fusion.49
  (212 shorter events, 45.9 us)
Async XLA Ops:
  6.5 160.4 %copy-start = (bf16[1,768,1024]{2,1,0:T(8,128)(2,1)S(1)}, bf16[1,768,1024]{2,1,0:T(8,128)(2,1)}, u32[]{:S(2)}) copy-start(bf16[1,768,1024]{2,1,0:T(8,128)(2,1)} %param.41) | copy-start | bytes 4718596
  6.5 100.7 %all-gather.3.cloned.1.call-start = ((), (), s32[]{:S(2)}) async-start(), calls=%async_computation.3 | async-start | bytes 1114112 | tf_op jit(solution)/shard_map/all_gather | solution.py:132
  6.5 60.0 %copy-start.5 = (s32[8,8]{1,0:T(8,128)S(1)}, s32[8,8]{1,0:T(8,128)}, u32[]{:S(2)}) copy-start(s32[8,8]{1,0:T(8,128)} %param.36) | copy-start | bytes 772
  6.5 60.1 %copy-start.9 = (u32[32]{0:T(128)S(1)}, u32[32]{0:T(128)}, u32[]{:S(2)}) copy-start(u32[32]{0:T(128)} %constant.109) | copy-start | bytes 388
  65.9 0.6 copy-start.3
  65.9 47.7 %copy-start.8 = (s32[16]{0:T(128)S(1)}, s32[16]{0:T(128)}, u32[]{:S(2)}) copy-start(s32[16]{0:T(128)} %param.38) | copy-start | bytes 196
  65.9 47.7 %copy-start.7 = (bf16[1024]{0:T(1024)(128)(2,1)S(1)}, bf16[1024]{0:T(1024)(128)(2,1)}, u32[]{:S(2)}) copy-start(bf16[1024]{0:T(1024)(128)(2,1)} %param.35) | copy-start | bytes 6148
  65.9 54.2 %copy-start.4 = (bf16[8,1024]{1,0:T(8,128)(2,1)S(1)}, bf16[8,1024]{1,0:T(8,128)(2,1)}, u32[]{:S(2)}) copy-start(bf16[8,1024]{1,0:T(8,128)(2,1)} %param.34) | copy-start | bytes 49156
  82.5 59.1 %copy-start.1 = (bf16[1,1024,768]{2,1,0:T(8,128)(2,1)S(1)}, bf16[1,1024,768]{2,1,0:T(8,128)(2,1)}, u32[]{:S(2)}) copy-start(bf16[1,1024,768]{2,1,0:T(8,128)(2,1)} %param.40) | copy-start | bytes 4718596
  109.8 10.3 %all-to-all-start = ((bf16[16,8,128]{2,1,0:T(8,128)(2,1)}), bf16[16,8,128]{2,1,0:T(8,128)(2,1)S(1)}, u32[]{:S(2)}, u32[]{:S(2)}) async-start(bf16[16,8,128]{2,1,0:T(8,128)(2,1)} %fusion.47), calls=%async_computation | async-start | bytes 65536 | tf_op jit(solution)/shard_map/all_to_all | solution.py:136
  113.5 53.5 %all-reduce.4.cloned.1.call-start = ((), (), s32[]{:S(2)}) async-start(), calls=%async_computation.4 | async-start | bytes 786432 | tf_op jit(solution)/shard_map/psum | solution.py:172
  128.6 14.1 %copy-start.2 = (bf16[1,1024,768]{2,1,0:T(8,128)(2,1)S(1)}, bf16[1,1024,768]{2,1,0:T(8,128)(2,1)}, u32[]{:S(2)}) copy-start(bf16[1,1024,768]{2,1,0:T(8,128)(2,1)} %param.39) | copy-start | bytes 4718596
  142.7 1.1 copy-start.6
  169.1 15.6 %all-to-all-start.2 = ((bf16[16,8,1024]{2,1,0:T(8,128)(2,1)}), bf16[16,8,1024]{2,1,0:T(8,128)(2,1)S(1)}, u32[]{:S(2)}, u32[]{:S(2)}) async-start(bf16[16,8,1024]{2,1,0:T(8,128)(2,1)} %fusion.44), calls=%async_computation.2 | async-start | bytes 524288 | tf_op jit(solution)/shard_map/all_to_all | solution.py:178
Sparse Core Ops, SparseCore 0:
  66.6 40.5 all-gather.2
  143.9 23.0 all-reduce.3
where the time goes:
time: 195 us; the launch traced here: 193 us
  waiting for transfers between devices  63.4 us (33%)
  blocking collectives  34.7 us (18%)
  local copies, waits for them, and re-layouts  31.9 us (16%)
  other arithmetic  25.8 us (13%)
  between operations  14.3 us (7%)
  matrix products  12.7 us (7%)
  starting transfers between devices  9.35 us (5%)
    all_gather x1, waiting for transfers between devices, shards(): lax.all_gather(attended, ('ep', 'sub'), axis=0, tiled=True)  24.7 us
    psum x1, waiting for transfers between devices, slot_sums(): lax.psum(up_sum.astype(jnp.bfloat16), 'tp').astype(jnp.float32)  23.1 us
    dynamic_slice x16, local copies, waits for them, and re-layouts, shards(): lax.map(attend_one, (queries, new_keys, new_values, key_codes, key_scale,...  16.2 us
    unnamed x1, blocking collectives  13.8 us
    all_to_all x1, blocking collectives, shards(): lax.all_to_all(outgoing, ('ep', 'sub'), split_axis=0, concat_axis=0, tile...  12.6 us
    all_to_all x1, waiting for transfers between devices, shards(): lax.all_to_all(expert_out.reshape(source_count, item_count, width), ('ep'...  9.72 us
    psum x1, blocking collectives, shards(): lax.psum(placed.astype(jnp.bfloat16), 'tp').astype(jnp.float32)  8.37 us
    shift_right_arithmetic x24, local copies, waits for them, and re-layouts, unpack_codes(): jnp.right_shift(packed_words[..., None, :], shifts[:, None])  6.44 us
  transfers between devices with their start and end apart: 4, of which 4 were waited for; matrix products, arithmetic and copies ran while one was open for 1% of the time, Pallas kernels for 0%

commit v1 on v0

--- a/solution.py
+++ b/solution.py
@@ -1,8 +1,11 @@
+import functools
 import math
 
 import jax
 import jax.numpy as jnp
 from jax import lax
+from jax.experimental import pallas as pl
+from jax.experimental.pallas import tpu as pltpu
 from jax.sharding import PartitionSpec as P
 
 EPS = 1e-06
@@ -191,9 +194,521 @@
     return (hidden_state + moe).astype(jnp.bfloat16)
 
 
+F32, BF16 = jnp.float32, jnp.bfloat16
+NT = (((1,), (1,)), ((), ()))
+LANES, ROWS = 128, 8
+
+
+def layer_kernel(
+    sizes,
+    queries,
+    new_keys,
+    new_values,
+    key_codes,
+    key_scale,
+    key_zero,
+    value_codes,
+    value_scale,
+    value_zero,
+    lengths,
+    out_weight_hbm,
+    residual,
+    norm_gain,
+    expert_ids,
+    route_weights,
+    capacity,
+    w_gate_hbm,
+    w_up_hbm,
+    w_down_hbm,
+    mixed,
+    out_weight,
+    w_gate,
+    w_up,
+    w_down,
+    stage,
+    att_send,
+    att_recv,
+    ids_send,
+    ids_recv,
+    res_recv,
+    proj_send,
+    proj_recv,
+    hidden,
+    norm_send,
+    norm_recv,
+    sums_own,
+    sums_send,
+    sums_recv,
+    back_send,
+    back_recv,
+    weight_sem,
+    att_ss,
+    att_rs,
+    ids_ss,
+    ids_rs,
+    res_ss,
+    res_rs,
+    proj_ss,
+    proj_rs,
+    norm_ss,
+    norm_rs,
+    sums_ss,
+    sums_rs,
+    back_ss,
+    back_rs,
+):
+    n_tp, n_sub, owners, slots, chunk = sizes
+    n_all = owners * n_tp
+    tp = lax.axis_index("tp")
+    me = lax.axis_index("ep") * n_sub + lax.axis_index("sub")
+    requests, heads, head_dim = queries.shape
+    kv_heads, words = key_codes.shape[1:3]
+    key_groups = key_scale.shape[2]
+    per_group = heads // kv_heads
+    tokens = owners * requests
+    quarter = residual.shape[1]
+    tiles = quarter // LANES
+    ff = w_gate.shape[1]
+    chunks = ff // chunk
+
+    def place(owner, t):
+        return {"ep": owner // n_sub, "sub": lax.rem(owner, n_sub), "tp": t}
+
+    def remote(src, dst, ss, rs, owner, t):
+        return pltpu.make_async_remote_copy(
+            src_ref=src,
+            dst_ref=dst,
+            send_sem=ss,
+            recv_sem=rs,
+            device_id=place(owner, t),
+            device_id_type=pl.DeviceIdType.MESH,
+        )
+
+    def loop(count, body):
+        def step(k, carry):
+            body(k)
+            return carry
+
+        lax.fori_loop(0, count, step, 0)
+
+    barrier = pltpu.get_barrier_semaphore()
+
+    def greet(k):
+        other = lax.rem(me * n_tp + tp + k + 1, n_all)
+        pl.semaphore_signal(
+            barrier,
+            inc=1,
+            device_id=place(other // n_tp, lax.rem(other, n_tp)),
+            device_id_type=pl.DeviceIdType.MESH,
+        )
+
+    loop(n_all - 1, greet)
+    loads = [
+        pltpu.make_async_copy(out_weight_hbm, out_weight, weight_sem.at[0]),
+        pltpu.make_async_copy(w_gate_hbm.at[0], w_gate, weight_sem.at[1]),
+        pltpu.make_async_copy(w_up_hbm.at[0], w_up, weight_sem.at[2]),
+        pltpu.make_async_copy(w_down_hbm.at[0], w_down, weight_sem.at[3]),
+    ]
+    for load in loads:
+        load.start()
+
+    ids = expert_ids[...]
+    raw = route_weights[...].astype(F32)
+    shares = raw / jnp.sum(raw, axis=1, keepdims=True)
+    lane = lax.broadcasted_iota(jnp.int32, (requests, LANES), 1)
+    named = jnp.zeros((requests, LANES), F32)
+    weight_per = jnp.zeros((requests, LANES), F32)
+    for k in range(ids.shape[1]):
+        hit = ids[:, k : k + 1] == lane
+        named = named + jnp.where(hit, 1.0, 0.0)
+        weight_per = weight_per + jnp.where(hit, shares[:, k : k + 1], 0.0)
+    ids_send[...] = named
+    ids_recv[me] = named
+    res_recv[tp] = residual[...]
+
+    def other_owner(k):
+        return lax.rem(me + k + 1, owners)
+
+    def other_tp(k):
+        return lax.rem(tp + k + 1, n_tp)
+
+    span = words * 16
+    row_at = lax.broadcasted_iota(jnp.int32, (span, span), 0)
+    col_at = lax.broadcasted_iota(jnp.int32, (span, span), 1)
+    moved = 16 * lax.rem(col_at, words) + col_at // words
+    perm = jnp.where(row_at == moved, 1.0, 0.0).astype(BF16)
+    shifts = 2 * lax.broadcasted_iota(jnp.int32, (16, words, head_dim), 0)
+    word_at = lax.broadcasted_iota(jnp.int32, (words, head_dim), 0)
+    lane_pos = lax.broadcasted_iota(jnp.int32, (per_group, span), 1)
+    position = 16 * lax.rem(lane_pos, words) + lane_pos // words
+    inv_scale = 1.0 / math.sqrt(head_dim)
+
+    def per_word(ref, b, g):
+        rows = ref[b, g].astype(F32)
+        out = rows[0:1, :] * jnp.ones((words, 1), F32)
+        for i in range(1, key_groups):
+            out = jnp.where(word_at >= i * (words // key_groups), rows[i : i + 1, :], out)
+        return out
+
+    v_steps = [
+        jnp.dot(value_scale[b], perm, preferred_element_type=F32) for b in range(requests)
+    ]
+    v_zeros = [jnp.dot(value_zero[b], perm, preferred_element_type=F32) for b in range(requests)]
+    for g in range(kv_heads):
+        scores, own_scores = [], []
+        for b in range(requests):
+            code = jnp.bitwise_and(jnp.right_shift(key_codes[b, g][None], shifts), 3).astype(F32)
+            keys = code * per_word(key_scale, b, g)[None] + per_word(key_zero, b, g)[None]
+            keys = keys.reshape(span, head_dim).astype(BF16)
+            q = queries[b, g * per_group : (g + 1) * per_group, :]
+            s = lax.dot_general(q, keys, NT, preferred_element_type=F32) * inv_scale
+            scores.append(jnp.where(position < lengths[b], s, -jnp.inf))
+            nk = new_keys[b, g : g + 1, :].astype(F32)
+            own_scores.append(jnp.sum(q.astype(F32) * nk, axis=1, keepdims=True) * inv_scale)
+        score = jnp.concatenate(scores, axis=0)
+        own = jnp.concatenate(own_scores, axis=0)
+        highest = jnp.maximum(jnp.max(score, axis=1, keepdims=True), own)
+        weights = jnp.exp(score - highest)
+        own_w = jnp.exp(own - highest)
+        inverse = 1.0 / (jnp.sum(weights, axis=1, keepdims=True) + own_w)
+        weights = weights * inverse
+        own_w = own_w * inverse
+        for b in range(requests):
+            p = weights[b * per_group : (b + 1) * per_group, :]
+            o = own_w[b * per_group : (b + 1) * per_group, :]
+            code = jnp.bitwise_and(jnp.right_shift(value_codes[b, g][None], shifts), 3)
+            code = code.astype(F32).reshape(span, head_dim).astype(BF16)
+            ps = (p * v_steps[b][g : g + 1, :]).astype(BF16)
+            res = jnp.dot(ps, code, preferred_element_type=F32)
+            res = res + jnp.sum(p * v_zeros[b][g : g + 1, :], axis=1, keepdims=True)
+            res = res + o * new_values[b, g : g + 1, :].astype(F32)
+            stage[g, pl.ds(b, per_group, stride=requests), :] = res
+        done = stage[g].astype(BF16)
+        att_send[g] = done
+        att_recv[me, g] = done
+        if g == 0:
+            pl.semaphore_wait(barrier, n_all - 1)
+
+        def send_att(k):
+            p = other_owner(k)
+            remote(
+                att_send.at[g], att_recv.at[me, g], att_ss.at[g, k], att_rs.at[g, me], p, tp
+            ).start()
+
+        loop(owners - 1, send_att)
+
+    def send_ids(k):
+        remote(ids_send, ids_recv.at[me], ids_ss.at[k], ids_rs.at[me], other_owner(k), tp).start()
+
+    def send_res(k):
+        remote(residual, res_recv.at[tp], res_ss.at[k], res_rs.at[tp], me, other_tp(k)).start()
+
+    loop(n_tp - 1, send_res)
+    loop(owners - 1, send_ids)
+
+    loads[0].wait()
+    spread = jnp.zeros((tokens, LANES), F32)
+    for g in range(kv_heads):
+
+        def got_att(k):
+            s = other_owner(k)
+            remote(
+                att_send.at[g], att_recv.at[s, g], att_ss.at[g, k], att_rs.at[g, s], s, tp
+            ).wait_recv()
+
+        loop(owners - 1, got_att)
+        got = att_recv[:, g].astype(F32).reshape(owners, per_group, requests, head_dim)
+        lhs = [got[:, h].reshape(tokens, head_dim).astype(BF16) for h in range(per_group)]
+        width = per_group * head_dim
+        spread = spread + jnp.dot(
+            jnp.concatenate(lhs, axis=1),
+            out_weight[g * width : (g + 1) * width, :],
+            preferred_element_type=F32,
+        )
+    proj_send[...] = spread.reshape(owners, requests, LANES).astype(BF16)
+    proj_recv[tp, me] = proj_send[me]
+
+    def pair(k):
+        other = lax.rem(me * n_tp + tp + k + 1, n_all)
+        return other // n_tp, lax.rem(other, n_tp)
+
+    def send_proj(k):
+        p, t = pair(k)
+        remote(
+            proj_send.at[p], proj_recv.at[tp, me], proj_ss.at[k], proj_rs.at[tp, me], p, t
+        ).start()
+
+    loop(n_all - 1, send_proj)
+
+    def got_ids(k):
+        s = other_owner(k)
+        remote(ids_send, ids_recv.at[s], ids_ss.at[k], ids_rs.at[s], s, tp).wait_recv()
+
+    loop(owners - 1, got_ids)
+    named_all = ids_recv[...].reshape(tokens, LANES)
+    before = lax.broadcasted_iota(jnp.int32, (tokens, tokens), 0) > lax.broadcasted_iota(
+        jnp.int32, (tokens, tokens), 1
+    )
+    rank = jnp.dot(
+        jnp.where(before, 1.0, 0.0).astype(BF16),
+        named_all.astype(BF16),
+        preferred_element_type=F32,
+    )
+    limit = capacity[me].astype(F32)
+    ranked = jnp.where((named_all > 0.5) & (rank < limit), rank, -1.0)
+    mine = lax.broadcasted_iota(jnp.int32, (tokens, LANES), 1) == me
+    rank_col = jnp.sum(jnp.where(mine, ranked, 0.0), axis=1, keepdims=True)
+    pick = jnp.where(lax.broadcasted_iota(jnp.int32, (ROWS, LANES), 1) == me, 1.0, 0.0)
+    rank_row = lax.dot_general(
+        pick.astype(BF16), ranked.astype(BF16), NT, preferred_element_type=F32
+    )[0:1, :]
+    slot_row = lax.broadcasted_iota(jnp.int32, (slots, tokens), 0).astype(F32)
+    slot_col = lax.broadcasted_iota(jnp.int32, (tokens, slots), 1).astype(F32)
+    packer = jnp.where(rank_row == slot_row, 1.0, 0.0).astype(BF16)
+    unpacker = jnp.where(rank_col == slot_col, 1.0, 0.0).astype(BF16)
+
+    def got_res(k):
+        t = other_tp(k)
+        remote(residual, res_recv.at[t], res_ss.at[k], res_rs.at[t], me, t).wait_recv()
+
+    loop(n_tp - 1, got_res)
+
+    def got_proj(k):
+        s, t = pair(k)
+        remote(
+            proj_send.at[s], proj_recv.at[t, s], proj_ss.at[k], proj_rs.at[t, s], s, t
+        ).wait_recv()
+
+    loop(n_all - 1, got_proj)
+    total = proj_recv[0].astype(F32)
+    for t in range(1, n_tp):
+        total = total + proj_recv[t].astype(F32)
+    squares = jnp.zeros((requests, LANES), F32)
+    for i in range(owners):
+        t, k = divmod(i, tiles)
+        h = total[i] + res_recv[t, :, k * LANES : (k + 1) * LANES].astype(F32)
+        hidden[t, k] = h
+        squares = squares + h * h
+    mean_square = jnp.sum(squares, axis=1, keepdims=True) * (1.0 / (owners * LANES))
+    inv_rms = lax.rsqrt(mean_square + EPS)
+    own_hidden = hidden[tp]
+    normed = [
+        own_hidden[k] * inv_rms * norm_gain[:, k * LANES : (k + 1) * LANES].astype(F32)
+        for k in range(tiles)
+    ]
+    normed = jnp.concatenate(normed, axis=0).astype(BF16)
+    norm_send[...] = normed
+    norm_recv[me] = normed
+
+    def send_norm(k):
+        remote(
+            norm_send, norm_recv.at[me], norm_ss.at[k], norm_rs.at[me], other_owner(k), tp
+        ).start()
+
+    loop(owners - 1, send_norm)
+    loads[1].wait()
+    loads[2].wait()
+    loads[3].wait()
+
+    def got_norm(k):
+        s = other_owner(k)
+        remote(norm_send, norm_recv.at[s], norm_ss.at[k], norm_rs.at[s], s, tp).wait_recv()
+
+    loop(owners - 1, got_norm)
+    got = norm_recv[...].astype(F32).reshape(owners, tiles, requests, LANES)
+    rows = [got[:, k].reshape(tokens, LANES).astype(BF16) for k in range(tiles)]
+    packed = jnp.dot(
+        packer, jnp.concatenate(rows, axis=1), preferred_element_type=F32
+    ).astype(BF16)
+    for c in range(chunks):
+        cols = slice(c * chunk, (c + 1) * chunk)
+        both = jnp.concatenate(
+            [
+                jnp.dot(packed, w_gate[:, cols], preferred_element_type=F32),
+                jnp.dot(packed, w_up[:, cols], preferred_element_type=F32),
+            ],
+            axis=1,
+        )
+        sums_own[c] = both
+        sums_send[c] = both.astype(BF16)
+
+        def send_sums(k):
+            remote(
+                sums_send.at[c],
+                sums_recv.at[tp, c],
+                sums_ss.at[c, k],
+                sums_rs.at[c, tp],
+                me,
+                other_tp(k),
+            ).start()
+
+        loop(n_tp - 1, send_sums)
+    expert_out = jnp.zeros((slots, quarter), F32)
+    for c in range(chunks):
+        both = sums_own[c]
+        for k in range(n_tp - 1):
+            t = other_tp(k)
+            remote(
+                sums_send.at[c], sums_recv.at[t, c], sums_ss.at[c, k], sums_rs.at[c, t], me, t
+            ).wait_recv()
+            both = both + sums_recv[t, c].astype(F32)
+        gate, up = both[:, :chunk], both[:, chunk:]
+        activated = (gate / (1.0 + jnp.exp(-gate)) * up).astype(BF16)
+        expert_out = expert_out + jnp.dot(
+            activated, w_down[c * chunk : (c + 1) * chunk, :], preferred_element_type=F32
+        )
+    spread_back = jnp.dot(unpacker, expert_out.astype(BF16), preferred_element_type=F32)
+    for r in range(owners):
+        part = [
+            spread_back[r * requests : (r + 1) * requests, k * LANES : (k + 1) * LANES]
+            for k in range(tiles)
+        ]
+        back_send[r] = jnp.concatenate(part, axis=0).astype(BF16)
+    back_recv[me] = back_send[me]
+
+    def send_back(k):
+        p = other_owner(k)
+        remote(
+            back_send.at[p], back_recv.at[me], back_ss.at[k], back_rs.at[me], p, tp
+        ).start()
+
+    loop(owners - 1, send_back)
+
+    def got_back(k):
+        s = other_owner(k)
+        remote(back_send.at[s], back_recv.at[s], back_ss.at[k], back_rs.at[s], s, tp).wait_recv()
+
+    loop(owners - 1, got_back)
+    moe = own_hidden
+    for e in range(owners):
+        part = back_recv[e].astype(F32).reshape(tiles, requests, LANES)
+        moe = moe + part * weight_per[:, e : e + 1][None]
+    for k in range(tiles):
+        mixed[:, k * LANES : (k + 1) * LANES] = moe[k].astype(BF16)
+
+    def sent_owner(k):
+        p = other_owner(k)
+        for g in range(kv_heads):
+            remote(
+                att_send.at[g], att_recv.at[me, g], att_ss.at[g, k], att_rs.at[g, me], p, tp
+            ).wait_send()
+        remote(ids_send, ids_recv.at[me], ids_ss.at[k], ids_rs.at[me], p, tp).wait_send()
+        remote(norm_send, norm_recv.at[me], norm_ss.at[k], norm_rs.at[me], p, tp).wait_send()
+        remote(
+            back_send.at[p], back_recv.at[me], back_ss.at[k], back_rs.at[me], p, tp
+        ).wait_send()
+
+    def sent_tp(k):
+        t = other_tp(k)
+        remote(residual, res_recv.at[tp], res_ss.at[k], res_rs.at[tp], me, t).wait_send()
+        for c in range(chunks):
+            remote(
+                sums_send.at[c], sums_recv.at[tp, c], sums_ss.at[c, k], sums_rs.at[c, tp], me, t
+            ).wait_send()
+
+    def sent_proj(k):
+        p, t = pair(k)
+        remote(
+            proj_send.at[p], proj_recv.at[tp, me], proj_ss.at[k], proj_rs.at[tp, me], p, t
+        ).wait_send()
+
+    loop(owners - 1, sent_owner)
+    loop(n_tp - 1, sent_tp)
+    loop(n_all - 1, sent_proj)
+
+
+def fused_shards(n_ep, n_tp, n_sub, *args):
+    owners = n_ep * n_sub
+    queries, key_codes, out_weight, residual = args[0], args[3], args[10], args[11]
+    norm_gain, expert_ids, capacity, w_gate, w_down = (
+        args[12],
+        args[13],
+        args[15],
+        args[16],
+        args[18],
+    )
+    requests, heads, head_dim = queries.shape
+    kv_heads = key_codes.shape[1]
+    quarter, ff = residual.shape[1], w_gate.shape[2]
+    tiles = quarter // LANES
+    tokens = owners * requests
+    slots = tokens * expert_ids.shape[1] // (2 * owners)
+    chunk = 256
+    chunks = ff // chunk
+    group_rows = heads // kv_heads * requests
+    vmem, dma = pltpu.VMEM, pltpu.SemaphoreType.DMA
+    in_vmem = pl.BlockSpec(memory_space=pltpu.VMEM)
+    in_smem = pl.BlockSpec(memory_space=pltpu.SMEM)
+    in_any = pl.BlockSpec(memory_space=pl.ANY)
+    specs = [in_vmem] * 9 + [in_smem, in_any] + [in_vmem] * 4 + [in_smem] + [in_any] * 3
+    args = list(args)
+    args[12] = norm_gain.reshape(1, -1)
+    return pl.pallas_call(
+        functools.partial(layer_kernel, (n_tp, n_sub, owners, slots, chunk)),
+        out_shape=jax.ShapeDtypeStruct(residual.shape, BF16),
+        in_specs=specs,
+        out_specs=in_vmem,
+        scratch_shapes=[
+            vmem(out_weight.shape, BF16),
+            vmem(w_gate.shape[1:], BF16),
+            vmem(w_gate.shape[1:], BF16),
+            vmem(w_down.shape[1:], BF16),
+            vmem((kv_heads, group_rows, head_dim), F32),
+            vmem((kv_heads, group_rows, head_dim), BF16),
+            vmem((owners, kv_heads, group_rows, head_dim), BF16),
+            vmem((requests, LANES), F32),
+            vmem((owners, requests, LANES), F32),
+            vmem((n_tp, requests, quarter), BF16),
+            vmem((owners, requests, LANES), BF16),
+            vmem((n_tp, owners, requests, LANES), BF16),
+            vmem((n_tp, tiles, requests, LANES), F32),
+            vmem((tiles * requests, LANES), BF16),
+            vmem((owners, tiles * requests, LANES), BF16),
+            vmem((chunks, slots, 2 * chunk), F32),
+            vmem((chunks, slots, 2 * chunk), BF16),
+            vmem((n_tp, chunks, slots, 2 * chunk), BF16),
+            vmem((owners, tiles * requests, LANES), BF16),
+            vmem((owners, tiles * requests, LANES), BF16),
+            dma((4,)),
+            dma((kv_heads, owners)),
+            dma((kv_heads, owners)),
+            dma((owners,)),
+            dma((owners,)),
+            dma((n_tp,)),
+            dma((n_tp,)),
+            dma((owners * n_tp,)),
+            dma((n_tp, owners)),
+            dma((owners,)),
+            dma((owners,)),
+            dma((chunks, n_tp)),
+            dma((chunks, n_tp)),
+            dma((owners,)),
+            dma((owners,)),
+        ],
+        compiler_params=pltpu.CompilerParams(collective_id=0, has_side_effects=True),
+    )(*args)
+
+
+def layer(n_ep, n_tp, n_sub, *args):
+    requests, heads, head_dim = args[0].shape
+    fits = (
+        requests == ROWS
+        and head_dim == LANES
+        and args[3].shape[2] * 16 == LANES
+        and (heads // args[3].shape[1]) % 16 == 0
+        and args[10].shape[1] == LANES
+        and args[11].shape[1] * n_tp == n_ep * n_sub * LANES
+        and args[16].shape[0] == 1
+        and n_ep * n_sub == args[15].shape[0]
+        and n_ep * n_sub * requests == LANES
+    )
+    return fused_shards(n_ep, n_tp, n_sub, *args) if fits else shards(*args)
+
+
 def solution(mesh):
+    sizes = [mesh.shape[axis] for axis in ("ep", "tp", "sub")]
     return jax.shard_map(
-        shards,
+        functools.partial(layer, *sizes),
         mesh=mesh,
         in_specs=(
             P(("groups", "ep", "sub"), "tp", None),

time: 195 us -> 63.1 us (0.32)
  waiting for transfers between devices: 63.4 us -> 0 us
  Pallas kernels: 0 us -> 60.3 us
  blocking collectives: 34.7 us -> 0 us
  local copies, waits for them, and re-layouts: 31.9 us -> 2.6 us
  other arithmetic: 25.8 us -> 0 us
  between operations: 14.3 us -> 0.01 us
  matrix products: 12.7 us -> 0 us
  starting transfers between devices: 9.35 us -> 0 us
    pallas_call x0 -> x1, Pallas kernels: none -> 60.3 us  [fused_shards(): pl.pallas_call(functools.partial(layer_kernel, (n_tp, n_sub, owners, slot...]
    all_gather x1 -> x0, waiting for transfers between devices: 24.7 us -> none  [shards(): lax.all_gather(attended, ('ep', 'sub'), axis=0, tiled=True)]
    psum x1 -> x0, waiting for transfers between devices: 23.1 us -> none  [slot_sums(): lax.psum(up_sum.astype(jnp.bfloat16), 'tp').astype(jnp.float32)]
    convert_element_type x36 -> x0, other arithmetic: 17.8 us -> none  [the longest x8 5.76 us: attend_one(): key_step.astype(jnp.float32)]
    dynamic_slice x16 -> x0, local copies, waits for them, and re-layouts: 16.2 us -> none  [shards(): lax.map(attend_one, (queries, new_keys, new_values, key_codes, key_scale,...]
    all_to_all x2 -> x0, waiting for transfers between devices: 15.6 us -> none  [the longest x1 9.72 us: shards(): lax.all_to_all(expert_out.reshape(source_count, item_count, width), ('ep'...]
    unnamed x1 -> x0, blocking collectives: 13.8 us -> none
    dot_general x30 -> x0, matrix products: 12.7 us -> none  [the longest x1 2.56 us: shards(): jnp.dot(lax.all_gather(attended, ('ep', 'sub'), axis=0, tiled=True), out_...]
  transfers between devices with their start and end apart: 4 -> 0, of which waited for: 4 -> 0; matrix products, arithmetic and copies ran while one was open for 1% -> 0% of each run, Pallas kernels for 0% -> 0%
where the time goes in v1:
time: 63.1 us; the launch traced here: 62.9 us
  Pallas kernels  60.3 us (96%)
  local copies, waits for them, and re-layouts  2.6 us (4%)
    pallas_call x1, Pallas kernels, fused_shards(): pl.pallas_call(functools.partial(layer_kernel, (n_tp, n_sub, owners, slot...  60.3 us
    unnamed x1, local copies, waits for them, and re-layouts  1.32 us
    reshape x1, local copies, waits for them, and re-layouts, fused_shards(): args[12] = norm_gain.reshape(1, -1)  1.28 us

profile of v1, /device:TPU:0, one launch (start us, length us, event | category | flops | bytes accessed | tf_op | source)
XLA Modules:
  0.0 62.9 jit_solution(11995901672751440656)
XLA Ops:
  0.0 1.3 %reshape.3.norm_gain = bf16[1,1024]{1,0:T(2,128)(2,1)} reshape(bf16[1024]{0:T(1024)(128)(2,1)} %param.31) | data formatting | bytes 4096 | tf_op jit(solution)/shard_map/reshape | solution.py:645
  1.3 60.3 %shard_map.181 = bf16[8,1024]{1,0:T(8,128)(2,1)} custom-call(bf16[8,32,128]{2,1,0:T(8,128)(2,1)} %queries.1, bf16[8,2,128]{2,1,0:T(2,128)(2,1)} %new_keys.1, bf16[8,2,128]{2,1,0:T(2,128)(2,1)} %new_values.1, s32[8,2,8,128]{3,2,1,0:T(8,128)} %key_codes.1, bf16[8,2,4,128]{3,2,1,0:T(4,128)(2,1)} %key_scale.1, bf16[8,2,4,128]{3,2,1,0:T(4,128)(2,1)} %key_zero.1, ...), custom_call_target="tpu_custom_call" | custom-call | tf_op jit(solution)/shard_map/pallas_call | solution.py:646
  61.5 1.3 %copy.21 = bf16[8,1024]{1,0:T(8,128)(2,1)} copy(bf16[8,1024]{1,0:T(8,128)(2,1)} %shard_map.181) | data formatting | bytes 32768

commit v2 on v1

--- a/solution.py
+++ b/solution.py
@@ -226,7 +226,6 @@
     w_up,
     w_down,
     stage,
-    att_send,
     att_recv,
     ids_send,
     ids_recv,
@@ -234,7 +233,6 @@
     proj_send,
     proj_recv,
     hidden,
-    norm_send,
     norm_recv,
     sums_own,
     sums_send,
@@ -332,6 +330,109 @@
     def other_tp(k):
         return lax.rem(tp + k + 1, n_tp)
 
+    drains = []
+
+    def finish():
+        for item in drains:
+            if isinstance(item, tuple):
+                loop(*item)
+            else:
+                item.wait_send()
+        for load in left:
+            load.wait()
+
+    left = list(loads)
+
+    near = 2 if (owners // n_sub) % 2 == 0 else 1
+    row = near * n_sub
+    far = owners // row
+    my_far, my_near, my_sub = me // row, lax.rem(me // n_sub, near), lax.rem(me, n_sub)
+
+    def owner_at(f, y, u):
+        return (
+            lax.rem(my_far + f, far) * row
+            + lax.rem(my_near + y, near) * n_sub
+            + lax.rem(my_sub + u, n_sub)
+        )
+
+    def hand_on(part, block, slot, target):
+        view, ss, rs = part
+        copy = remote(view(block), view(block), ss(slot), rs(block), target, tp)
+        copy.start()
+        drains.append(copy)
+
+    def arrived(part, block):
+        view, ss, rs = part
+        remote(view(block), view(block), ss(0), rs(block), block, tp).wait_recv()
+
+    def start_gather(part):
+        for u in range(1, n_sub):
+            hand_on(part, me, far - 1 + u - 1, owner_at(0, 0, u))
+        for f in range(1, far):
+            hand_on(part, me, f - 1, owner_at(f, 0, 0))
+        for y in range(1, near):
+            hand_on(part, me, far - 1 + n_sub - 1 + y - 1, owner_at(0, y, 0))
+
+    def finish_gather(parts):
+        slot = far - 1 + n_sub - 1 + near - 1
+        for f in range(1, far):
+            for part in parts:
+                block = owner_at(f, 0, 0)
+                arrived(part, block)
+                for y in range(1, near):
+                    hand_on(part, block, slot + (f - 1) * (near - 1) + y - 1, owner_at(0, y, 0))
+        slot = slot + (far - 1) * (near - 1)
+        for f in range(0, far):
+            for y in range(0, near):
+                if f == 0 and y == 0:
+                    continue
+                for part in parts:
+                    block = owner_at(f, y, 0)
+                    if y > 0:
+                        arrived(part, block)
+                    for u in range(1, n_sub):
+                        hand_on(
+                            part,
+                            block,
+                            slot + (f * near + y - 1) * (n_sub - 1) + u - 1,
+                            owner_at(0, 0, u),
+                        )
+        for f in range(0, far):
+            for y in range(0, near):
+                for u in range(1, n_sub):
+                    for part in parts:
+                        arrived(part, owner_at(f, y, u))
+
+    def start_near(part):
+        for u in range(1, n_sub):
+            hand_on(part, me, u - 1, owner_at(0, 0, u))
+        for j in range(1, far * near):
+            hand_on(part, me, n_sub - 1 + j - 1, owner_at(j // near, j % near, 0))
+
+    def finish_near(part):
+        slot = n_sub - 1 + far * near - 1
+        for j in range(1, far * near):
+            block = owner_at(j // near, j % near, 0)
+            arrived(part, block)
+            for u in range(1, n_sub):
+                hand_on(part, block, slot + (j - 1) * (n_sub - 1) + u - 1, owner_at(0, 0, u))
+        for j in range(far * near):
+            for u in range(1, n_sub):
+                arrived(part, owner_at(j // near, j % near, u))
+
+    def att_part(g):
+        return (
+            lambda block: att_recv.at[block, g],
+            lambda slot: att_ss.at[g, slot],
+            lambda block: att_rs.at[g, block],
+        )
+
+    norm_part = (
+        lambda block: norm_recv.at[block],
+        lambda slot: norm_ss.at[slot],
+        lambda block: norm_rs.at[block],
+    )
+
     span = words * 16
     row_at = lax.broadcasted_iota(jnp.int32, (span, span), 0)
     col_at = lax.broadcasted_iota(jnp.int32, (span, span), 1)
@@ -383,19 +484,11 @@
             res = res + jnp.sum(p * v_zeros[b][g : g + 1, :], axis=1, keepdims=True)
             res = res + o * new_values[b, g : g + 1, :].astype(F32)
             stage[g, pl.ds(b, per_group, stride=requests), :] = res
-        done = stage[g].astype(BF16)
-        att_send[g] = done
-        att_recv[me, g] = done
+        att_recv[me, g] = stage[g].astype(BF16)
         if g == 0:
             pl.semaphore_wait(barrier, n_all - 1)
 
-        def send_att(k):
-            p = other_owner(k)
-            remote(
-                att_send.at[g], att_recv.at[me, g], att_ss.at[g, k], att_rs.at[g, me], p, tp
-            ).start()
-
-        loop(owners - 1, send_att)
+        start_gather(att_part(g))
 
     def send_ids(k):
         remote(ids_send, ids_recv.at[me], ids_ss.at[k], ids_rs.at[me], other_owner(k), tp).start()
@@ -406,17 +499,20 @@
     loop(n_tp - 1, send_res)
     loop(owners - 1, send_ids)
 
-    loads[0].wait()
+    def sent_res(k):
+        t = other_tp(k)
+        remote(residual, res_recv.at[tp], res_ss.at[k], res_rs.at[tp], me, t).wait_send()
+
+    def sent_ids(k):
+        p = other_owner(k)
+        remote(ids_send, ids_recv.at[me], ids_ss.at[k], ids_rs.at[me], p, tp).wait_send()
+
+    drains += [(n_tp - 1, sent_res), (owners - 1, sent_ids)]
+
+    left.pop(0).wait()
     spread = jnp.zeros((tokens, LANES), F32)
+    finish_gather([att_part(g) for g in range(kv_heads)])
     for g in range(kv_heads):
-
-        def got_att(k):
-            s = other_owner(k)
-            remote(
-                att_send.at[g], att_recv.at[s, g], att_ss.at[g, k], att_rs.at[g, s], s, tp
-            ).wait_recv()
-
-        loop(owners - 1, got_att)
         got = att_recv[:, g].astype(F32).reshape(owners, per_group, requests, head_dim)
         lhs = [got[:, h].reshape(tokens, head_dim).astype(BF16) for h in range(per_group)]
         width = per_group * head_dim
@@ -439,6 +535,14 @@
         ).start()
 
     loop(n_all - 1, send_proj)
+
+    def sent_proj(k):
+        p, t = pair(k)
+        remote(
+            proj_send.at[p], proj_recv.at[tp, me], proj_ss.at[k], proj_rs.at[tp, me], p, t
+        ).wait_send()
+
+    drains.append((n_all - 1, sent_proj))
 
     def got_ids(k):
         s = other_owner(k)
@@ -493,28 +597,16 @@
     inv_rms = lax.rsqrt(mean_square + EPS)
     own_hidden = hidden[tp]
     normed = [
-        own_hidden[k] * inv_rms * norm_gain[:, k * LANES : (k + 1) * LANES].astype(F32)
+        own_hidden[k] * inv_rms * norm_gain[pl.ds(k * LANES, LANES)].astype(F32)[None]
         for k in range(tiles)
     ]
     normed = jnp.concatenate(normed, axis=0).astype(BF16)
-    norm_send[...] = normed
     norm_recv[me] = normed
-
-    def send_norm(k):
-        remote(
-            norm_send, norm_recv.at[me], norm_ss.at[k], norm_rs.at[me], other_owner(k), tp
-        ).start()
-
-    loop(owners - 1, send_norm)
-    loads[1].wait()
-    loads[2].wait()
-    loads[3].wait()
-
-    def got_norm(k):
-        s = other_owner(k)
-        remote(norm_send, norm_recv.at[s], norm_ss.at[k], norm_rs.at[s], s, tp).wait_recv()
-
-    loop(owners - 1, got_norm)
+    start_near(norm_part)
+    while left:
+        left.pop(0).wait()
+
+    finish_near(norm_part)
     got = norm_recv[...].astype(F32).reshape(owners, tiles, requests, LANES)
     rows = [got[:, k].reshape(tokens, LANES).astype(BF16) for k in range(tiles)]
     packed = jnp.dot(
@@ -543,6 +635,18 @@
             ).start()
 
         loop(n_tp - 1, send_sums)
+
+        def sent_sums(k, c=c):
+            remote(
+                sums_send.at[c],
+                sums_recv.at[tp, c],
+                sums_ss.at[c, k],
+                sums_rs.at[c, tp],
+                me,
+                other_tp(k),
+            ).wait_send()
+
+        drains.append((n_tp - 1, sent_sums))
     expert_out = jnp.zeros((slots, quarter), F32)
     for c in range(chunks):
         both = sums_own[c]
@@ -574,6 +678,14 @@
 
     loop(owners - 1, send_back)
 
+    def sent_back(k):
+        p = other_owner(k)
+        remote(
+            back_send.at[p], back_recv.at[me], back_ss.at[k], back_rs.at[me], p, tp
+        ).wait_send()
+
+    drains.append((owners - 1, sent_back))
+
     def got_back(k):
         s = other_owner(k)
         remote(back_send.at[s], back_recv.at[s], back_ss.at[k], back_rs.at[s], s, tp).wait_recv()
@@ -586,35 +698,7 @@
     for k in range(tiles):
         mixed[:, k * LANES : (k + 1) * LANES] = moe[k].astype(BF16)
 
-    def sent_owner(k):
-        p = other_owner(k)
-        for g in range(kv_heads):
-            remote(
-                att_send.at[g], att_recv.at[me, g], att_ss.at[g, k], att_rs.at[g, me], p, tp
-            ).wait_send()
-        remote(ids_send, ids_recv.at[me], ids_ss.at[k], ids_rs.at[me], p, tp).wait_send()
-        remote(norm_send, norm_recv.at[me], norm_ss.at[k], norm_rs.at[me], p, tp).wait_send()
-        remote(
-            back_send.at[p], back_recv.at[me], back_ss.at[k], back_rs.at[me], p, tp
-        ).wait_send()
-
-    def sent_tp(k):
-        t = other_tp(k)
-        remote(residual, res_recv.at[tp], res_ss.at[k], res_rs.at[tp], me, t).wait_send()
-        for c in range(chunks):
-            remote(
-                sums_send.at[c], sums_recv.at[tp, c], sums_ss.at[c, k], sums_rs.at[c, tp], me, t
-            ).wait_send()
-
-    def sent_proj(k):
-        p, t = pair(k)
-        remote(
-            proj_send.at[p], proj_recv.at[tp, me], proj_ss.at[k], proj_rs.at[tp, me], p, t
-        ).wait_send()
-
-    loop(owners - 1, sent_owner)
-    loop(n_tp - 1, sent_tp)
-    loop(n_all - 1, sent_proj)
+    finish()
 
 
 def fused_shards(n_ep, n_tp, n_sub, *args):
@@ -641,8 +725,6 @@
     in_smem = pl.BlockSpec(memory_space=pltpu.SMEM)
     in_any = pl.BlockSpec(memory_space=pl.ANY)
     specs = [in_vmem] * 9 + [in_smem, in_any] + [in_vmem] * 4 + [in_smem] + [in_any] * 3
-    args = list(args)
-    args[12] = norm_gain.reshape(1, -1)
     return pl.pallas_call(
         functools.partial(layer_kernel, (n_tp, n_sub, owners, slots, chunk)),
         out_shape=jax.ShapeDtypeStruct(residual.shape, BF16),
@@ -654,7 +736,6 @@
             vmem(w_gate.shape[1:], BF16),
             vmem(w_down.shape[1:], BF16),
             vmem((kv_heads, group_rows, head_dim), F32),
-            vmem((kv_heads, group_rows, head_dim), BF16),
             vmem((owners, kv_heads, group_rows, head_dim), BF16),
             vmem((requests, LANES), F32),
             vmem((owners, requests, LANES), F32),
@@ -662,7 +743,6 @@
             vmem((owners, requests, LANES), BF16),
             vmem((n_tp, owners, requests, LANES), BF16),
             vmem((n_tp, tiles, requests, LANES), F32),
-            vmem((tiles * requests, LANES), BF16),
             vmem((owners, tiles * requests, LANES), BF16),
             vmem((chunks, slots, 2 * chunk), F32),
             vmem((chunks, slots, 2 * chunk), BF16),

time: 63.1 us -> 47.2 us (0.75)
  Pallas kernels: 60.3 us -> 45.3 us
  local copies, waits for them, and re-layouts: 2.6 us -> 1.32 us
    pallas_call x1, Pallas kernels: 60.3 us -> 45.3 us  [fused_shards(): pl.pallas_call(functools.partial(layer_kernel, (n_tp, n_sub, owners, slot...]
    reshape x1 -> x0, local copies, waits for them, and re-layouts: 1.28 us -> none  [fused_shards(): args[12] = norm_gain.reshape(1, -1)]
where the time goes in v2:
time: 47.2 us; the launch traced here: 46.6 us
  Pallas kernels  45.3 us (96%)
  local copies, waits for them, and re-layouts  1.32 us (3%)
    pallas_call x1, Pallas kernels, fused_shards(): pl.pallas_call(functools.partial(layer_kernel, (n_tp, n_sub, owners, slot...  45.3 us
    unnamed x1, local copies, waits for them, and re-layouts  1.32 us

profile of v2, /device:TPU:0, one launch (start us, length us, event | category | flops | bytes accessed | tf_op | source)
XLA Modules:
  0.0 46.6 jit_solution(3992060812689270352)
XLA Ops:
  0.0 45.3 %shard_map.181 = bf16[8,1024]{1,0:T(8,128)(2,1)} custom-call(bf16[8,32,128]{2,1,0:T(8,128)(2,1)} %queries.1, bf16[8,2,128]{2,1,0:T(2,128)(2,1)} %new_keys.1, bf16[8,2,128]{2,1,0:T(2,128)(2,1)} %new_values.1, s32[8,2,8,128]{3,2,1,0:T(8,128)} %key_codes.1, bf16[8,2,4,128]{3,2,1,0:T(4,128)(2,1)} %key_scale.1, bf16[8,2,4,128]{3,2,1,0:T(4,128)(2,1)} %key_zero.1, ...), custom_call_target="tpu_custom_call" | custom-call | tf_op jit(solution)/shard_map/pallas_call | solution.py:728
  45.3 1.3 %copy.21 = bf16[8,1024]{1,0:T(8,128)(2,1)} copy(bf16[8,1024]{1,0:T(8,128)(2,1)} %shard_map.181) | data formatting | bytes 32768
